TPU v7x, 32 devices: a whole 2x2x4 slice. The times are simulated.
32 devices in a mesh: tok: 4 (over z), out: 4 (over x, core), grp: 2 (over y).
Axes of the slice: x: 2, y: 2, z: 4, core: 2. Of those that a mesh axis runs over, the one named last changes fastest.
Arguments:
- activations: bfloat16 [1024, 2, 2048], P(('tok', 'grp'), None, 'out'), may hold values from -16 to 16
- out_grads: bfloat16 [1024, 2, 2048], P(('tok', 'grp'), None, 'out'), may hold values from -16 to 16
- weight: bfloat16 [2, 2048, 4096], P(None, 'out'), may hold values from -0.09375 to 0.09375
Outputs:
- update: bfloat16 [4096, 2, 2048], P(('tok', 'grp'), None, 'out')
- input_grad: bfloat16 [1024, 2, 2048], P(('tok', 'grp'), None, 'out')
All inputs are finite; a program needn't handle non-finite values.
Results may differ from a plain program's by a relative error of at most 0.0092.
Values may be sent and summed in bfloat16 or wider, within the bound.
A program may use at most 64 MiB of HBM per device.

v0:
```python
import math
import jax
import jax.numpy as jnp
from jax import lax
from jax.sharding import PartitionSpec as P

POWER = 3
DAMPING = 0.1
HIGH = lax.Precision.HIGHEST


def spread(piece):
    return lax.all_gather(piece, "out", axis=2, tiled=True)


def token_sums(maker, rows):
    return lax.psum_scatter(
        maker(jnp.int32(0), rows * lax.axis_size(("tok", "grp"))),
        ("tok", "grp"),
        scatter_dimension=0,
        tiled=True,
    )


def shared_rows(piece):
    return lax.all_gather(piece, ("tok", "grp"), axis=0, tiled=True)


def shared_total(vector):
    return lax.psum(vector, ("tok", "out", "grp"))


def diagonal_mask(rows, width, row_start, col_start):
    row_ids = row_start + lax.broadcasted_iota(jnp.int32, (rows, 1, width), 0)
    col_ids = col_start + lax.broadcasted_iota(jnp.int32, (rows, 1, width), 2)
    return jnp.where(row_ids == col_ids, 1.0, 0.0).astype(jnp.float32)


def multiply(left, right, gather_columns):
    row_band = spread(left)
    column_band = gather_columns(right)
    return jnp.einsum("rkj,jkc->rkc", row_band, column_band, preferred_element_type=jnp.float32)


def inverse_roots(tile, row_start, col_start, gather_columns, total):
    rows, count, width = tile.shape
    block = width * lax.axis_size("out")
    mask = diagonal_mask(rows, width, row_start, col_start)
    vector = jnp.ones((count, block), jnp.float32)
    image = vector
    for step in range(POWER):
        columns = lax.dynamic_slice_in_dim(vector, col_start, width, 1)
        part = jnp.einsum("rkc,kc->kr", tile, columns, precision=HIGH)
        placed = lax.dynamic_update_slice_in_dim(
            jnp.zeros((count, block), jnp.float32), part, row_start, 1
        )
        image = total(placed)
        if step + 1 < POWER:
            vector = image / jnp.sqrt(jnp.sum(image * image, axis=1, keepdims=True))
    scale = jnp.sum(vector * image, axis=1) / jnp.sum(vector * vector, axis=1)
    start = tile / scale[None, :, None]
    start_low = start.astype(jnp.bfloat16)
    first_low = ((3.0 * mask - start) / 2.0).astype(jnp.bfloat16)
    square_low = multiply(first_low, first_low, gather_columns).astype(jnp.bfloat16)
    moved = multiply(square_low, start_low, gather_columns)
    second_low = ((3.0 * mask - moved) / 2.0).astype(jnp.bfloat16)
    roots = multiply(first_low, second_low, gather_columns) / jnp.sqrt(scale)[None, :, None]
    return roots.astype(jnp.bfloat16)


def local(activations, out_grads, weight):
    tok_dev, blocks, width = activations.shape
    block = width * lax.axis_size("out")
    token_count = tok_dev * lax.axis_size("tok") * lax.axis_size("grp")
    col_start = lax.axis_index("out") * width
    local_sides = jnp.concatenate([activations, out_grads], axis=1)
    whole_sides = spread(local_sides)
    grads_whole = whole_sides[:, blocks:, :]
    weight_rows = weight.reshape(blocks, width, blocks, block)
    input_grad = jnp.einsum(
        "tjq,bcjq->tbc", grads_whole, weight_rows, preferred_element_type=jnp.float32
    ).astype(jnp.bfloat16)
    rows = block // (lax.axis_size("tok") * lax.axis_size("grp"))
    row_start = lax.axis_index(("tok", "grp")) * rows

    def shared_terms(start, span):
        return jnp.einsum(
            "tkr,tkc->rkc", whole_sides, local_sides, preferred_element_type=jnp.float32
        )

    sums = token_sums(shared_terms, rows)
    tile = sums / token_count + DAMPING * diagonal_mask(rows, width, row_start, col_start)
    roots = inverse_roots(tile, row_start, col_start, shared_rows, shared_total)
    bands = shared_rows(roots)
    whitened = jnp.einsum(
        "tkj,jkc->tkc", whole_sides, bands, preferred_element_type=jnp.float32
    ).astype(jnp.bfloat16)
    acts_whole = spread(whitened[:, :blocks, :]).reshape(tok_dev, blocks * block)
    grads_low = whitened[:, blocks:, :]
    owned_acts = lax.all_to_all(acts_whole, ("tok", "grp"), split_axis=1, concat_axis=0, tiled=True)
    update = jnp.einsum(
        "ta,tbc->abc",
        owned_acts,
        lax.all_gather(grads_low, ("tok", "grp"), axis=0, tiled=True),
        preferred_element_type=jnp.float32,
    )
    update = (update / math.sqrt(token_count)).astype(jnp.bfloat16)
    return (update, input_grad)


def solution(mesh):
    in_specs = (
        P(("tok", "grp"), None, "out"),
        P(("tok", "grp"), None, "out"),
        P(None, "out", None),
    )
    out_specs = (P(("tok", "grp"), None, "out"), P(("tok", "grp"), None, "out"))
    return jax.shard_map(local, mesh=mesh, in_specs=in_specs, out_specs=out_specs, check_vma=False)
```

profile of v0, /device:TPU:0, one launch (start us, length us, event | category | flops | bytes accessed | tf_op | source)
XLA Modules:
  0.0 1136.9 jit_solution(8817919165431428209)
XLA Ops:
  7.2 0.0 all-gather.10.cloned.1.call-start
  7.2 1.0 copy_dynamic-update-slice_fusion.1
  8.2 1.0 copy_dynamic-update-slice_fusion
  9.2 0.0 copy-start.1
  9.2 0.8 copy-done.1
  10.0 0.0 all-gather.10.cloned.1.call-update
  10.0 0.0 reduce-scatter.2.cloned.1.call-start
  10.0 25.4 %all-gather.10.cloned.1.call-done = bf16[128,4,2048]{2,0,1:T(8,128)(2,1)} async-done(((bf16[128,4,512]{2,0,1:T(8,128)(2,1)}), bf16[128,4,2048]{2,0,1:T(8,128)(2,1)}) %all-gather.10.cloned.1.call-update) | async-done | bytes 2097168 | tf_op jit(solution)/shard_map/all_gather | solution.py:13
  35.4 9.9 convolution_bitcast_fusion
  45.3 0.0 reduce-scatter.2.cloned.1.call-update
  45.3 0.0 all-gather.16.cloned.1.call-start
  45.4 0.1 select_multiply_fusion.1
  45.6 280.1 %reduce-scatter.2.cloned.1.call-done = f32[256,4,512]{0,2,1:T(8,128)} async-done(((f32[2048,4,512]{0,2,1:T(8,128)}), f32[256,4,512]{0,2,1:T(8,128)}) %reduce-scatter.2.cloned.1.call-update) | async-done | bytes 2097168 | tf_op jit(solution)/shard_map/reduce_scatter | solution.py:17
  325.7 0.0 copy-start
  325.7 3.0 fusion.10
  328.7 39.4 %psum.21 = f32[4,2048]{1,0:T(4,128)S(1)} all-reduce(f32[4,2048]{1,0:T(4,128)S(1)} %bitcast_dynamic-update-slice_fusion.2), channel_id=1, replica_groups=mesh['tok'=4,'out'=4,'grp'=2] {'tok','out','grp'}, use_global_device_ids=true, to_apply=%region_1.2 | all-reduce | flops 8192 | bytes 65536 | tf_op jit(solution)/shard_map/psum | solution.py:30
  368.2 0.1 multiply_reduce_fusion.3
  368.3 0.1 fusion.26
  368.4 0.0 copy-done
  368.4 1.3 fusion.9
  369.8 39.9 %psum.22 = f32[4,2048]{1,0:T(4,128)S(1)} all-reduce(f32[4,2048]{1,0:T(4,128)S(1)} %bitcast_dynamic-update-slice_fusion.1), channel_id=1, replica_groups=mesh['tok'=4,'out'=4,'grp'=2] {'tok','out','grp'}, use_global_device_ids=true, to_apply=%region_3.4 | all-reduce | flops 8192 | bytes 65536 | tf_op jit(solution)/shard_map/psum | solution.py:30
  409.7 0.1 multiply_reduce_fusion.2
  409.9 0.1 broadcast_divide_fusion
  409.9 1.3 fusion.8
  411.3 40.3 %psum.23 = f32[4,2048]{1,0:T(4,128)S(1)} all-reduce(f32[4,2048]{1,0:T(4,128)S(1)} %bitcast_dynamic-update-slice_fusion), channel_id=1, replica_groups=mesh['tok'=4,'out'=4,'grp'=2] {'tok','out','grp'}, use_global_device_ids=true, to_apply=%region_5.6 | all-reduce | flops 8192 | bytes 65536 | tf_op jit(solution)/shard_map/psum | solution.py:30
  451.6 0.2 multiply_reduce_fusion
  451.8 1.8 multiply_convert_fusion.1
  453.6 0.0 all-gather.16.cloned.1.call-update
  453.6 0.0 all-gather.14.cloned.1.call-start
  453.7 0.5 all-gather.14.cloned.1.call-update
  454.2 0.0 all-gather.12.cloned.1.call-start
  454.2 0.5 all-gather.12.cloned.1.call-update
  454.8 0.0 all-gather.18.cloned.1.call-start
  454.8 33.2 %all-gather.16.cloned.1.call-done = bf16[256,4,2048]{0,2,1:T(8,128)(2,1)} async-done(((bf16[256,4,512]{0,2,1:T(8,128)(2,1)}), bf16[256,4,2048]{0,2,1:T(8,128)(2,1)}) %all-gather.16.cloned.1.call-update) | async-done | bytes 4194320 | tf_op jit(solution)/shard_map/all_gather | solution.py:13
  488.0 127.4 %all-gather.14.cloned.1.call-done = bf16[2048,4,512]{0,2,1:T(8,128)(2,1)} async-done(((bf16[256,4,512]{0,2,1:T(8,128)(2,1)}), bf16[2048,4,512]{0,2,1:T(8,128)(2,1)}) %all-gather.14.cloned.1.call-update) | async-done | bytes 8388624 | tf_op jit(solution)/shard_map/all_gather | solution.py:26
  615.5 7.9 fusion.5
  623.3 0.0 all-gather.18.cloned.1.call-update
  623.4 0.2 all-gather.20.cloned.1.call-start
  623.6 116.9 %all-gather.12.cloned.1.call-done = bf16[2048,4,512]{0,2,1:T(8,128)(2,1)} async-done(((bf16[256,4,512]{0,2,1:T(8,128)(2,1)}), bf16[2048,4,512]{0,2,1:T(8,128)(2,1)}) %all-gather.12.cloned.1.call-update) | async-done | bytes 8388624 | tf_op jit(solution)/shard_map/all_gather | solution.py:26
  740.5 34.7 %all-gather.18.cloned.1.call-done = bf16[256,4,2048]{0,2,1:T(8,128)(2,1)} async-done(((bf16[256,4,512]{0,2,1:T(8,128)(2,1)}), bf16[256,4,2048]{0,2,1:T(8,128)(2,1)}) %all-gather.18.cloned.1.call-update) | async-done | bytes 4194320 | tf_op jit(solution)/shard_map/all_gather | solution.py:13
  775.2 7.9 fusion.4
  783.0 0.0 all-gather.20.cloned.1.call-update
  783.1 0.0 all-gather.22.cloned.1.call-start
  783.1 125.0 %all-gather.20.cloned.1.call-done = bf16[2048,4,512]{0,2,1:T(8,128)(2,1)} async-done(((bf16[256,4,512]{0,2,1:T(8,128)(2,1)}), bf16[2048,4,512]{0,2,1:T(8,128)(2,1)}) %all-gather.20.cloned.1.call-update) | async-done | bytes 8388624 | tf_op jit(solution)/shard_map/all_gather | solution.py:26
  908.2 8.0 fusion.6
  916.2 0.0 all-gather.22.cloned.1.call-update
  916.2 0.0 all-gather.24.cloned.1.call-start
  916.3 123.2 %all-gather.22.cloned.1.call-done = bf16[2048,4,512]{0,2,1:T(8,128)(2,1)} async-done(((bf16[256,4,512]{0,2,1:T(8,128)(2,1)}), bf16[2048,4,512]{0,2,1:T(8,128)(2,1)}) %all-gather.22.cloned.1.call-update) | async-done | bytes 8388624 | tf_op jit(solution)/shard_map/all_gather | solution.py:26
  1039.5 0.0 copy-done.2
  1039.5 5.7 fusion.11
  1045.2 0.8 fusion.34
  1046.0 0.0 all-gather.24.cloned.1.call-update
  1046.1 0.0 all-gather.26.cloned.1.call-start
  1046.1 0.5 all-gather.26.cloned.1.call-update
  1046.6 14.4 %all-gather.24.cloned.1.call-done = bf16[128,2,2048]{0,2,1:T(8,128)(2,1)} async-done(((bf16[128,2,512]{0,2,1:T(8,128)(2,1)}), bf16[128,2,2048]{0,2,1:T(8,128)(2,1)}) %all-gather.24.cloned.1.call-update) | async-done | bytes 1048592 | tf_op jit(solution)/shard_map/all_gather | solution.py:13
  1061.1 5.5 all-to-all-start
  1066.6 6.3 fusion.15
  1072.9 1.0 copy.20
  1073.8 27.3 %all-to-all-done = bf16[128,8,512]{0,2,1:T(8,128)(2,1)S(1)} async-done(((bf16[128,8,512]{0,2,1:T(8,128)(2,1)}), bf16[128,8,512]{0,2,1:T(8,128)(2,1)S(1)}, u32[]{:S(2)}, u32[]{:S(2)}) %all-to-all-start) | async-done | bytes 1048608 | tf_op jit(solution)/shard_map/all_to_all | solution.py:100
  1101.2 0.7 copy.16
  1101.9 0.5 reshape.81
  1102.4 22.7 %all-gather.26.cloned.1.call-done = bf16[1024,2,512]{0,2,1:T(8,128)(2,1)} async-done(((bf16[128,2,512]{0,2,1:T(8,128)(2,1)}), bf16[1024,2,512]{0,2,1:T(8,128)(2,1)}) %all-gather.26.cloned.1.call-update) | async-done | bytes 2097168 | tf_op jit(solution)/shard_map/all_gather | solution.py:104
  1125.1 2.9 multiply_convert_fusion
  1128.0 2.0 copy.19
  (13 shorter events, 0.1 us)
Async XLA Ops:
  7.2 28.3 %all-gather.10.cloned.1.call-start = ((), (), s32[]{:S(2)}) async-start(), calls=%async_computation.2 | async-start | bytes 2621440 | tf_op jit(solution)/shard_map/all_gather | solution.py:13
  9.2 0.8 copy-start.1
  10.0 315.7 %reduce-scatter.2.cloned.1.call-start = ((), (), s32[]{:S(2)}) async-start(), calls=%async_computation.3 | async-start | bytes 18874368 | tf_op jit(solution)/shard_map/reduce_scatter | solution.py:17
  45.3 442.7 %all-gather.16.cloned.1.call-start = ((), (), s32[]{:S(2)}) async-start(), calls=%async_computation.6 | async-start | bytes 5242880 | tf_op jit(solution)/shard_map/all_gather | solution.py:13
  325.7 42.7 %copy-start = (f32[256,4,512]{0,2,1:T(8,128)S(1)}, f32[256,4,512]{0,2,1:T(8,128)}, u32[]{:S(2)}) copy-start(f32[256,4,512]{0,2,1:T(8,128)} %reduce-scatter.2.cloned.1.call-done) | copy-start | bytes 6291460
  453.6 161.9 %all-gather.14.cloned.1.call-start = ((), (), s32[]{:S(2)}) async-start(), calls=%async_computation.5 | async-start | bytes 9437184 | tf_op jit(solution)/shard_map/all_gather | solution.py:26
  454.2 286.3 %all-gather.12.cloned.1.call-start = ((), (), s32[]{:S(2)}) async-start(), calls=%async_computation.4 | async-start | bytes 9437184 | tf_op jit(solution)/shard_map/all_gather | solution.py:26
  454.8 320.4 %all-gather.18.cloned.1.call-start = ((), (), s32[]{:S(2)}) async-start(), calls=%async_computation.7 | async-start | bytes 5242880 | tf_op jit(solution)/shard_map/all_gather | solution.py:13
  623.4 284.8 %all-gather.20.cloned.1.call-start = ((), (), s32[]{:S(2)}) async-start(), calls=%async_computation.8 | async-start | bytes 9437184 | tf_op jit(solution)/shard_map/all_gather | solution.py:26
  783.1 256.4 %all-gather.22.cloned.1.call-start = ((), (), s32[]{:S(2)}) async-start(), calls=%async_computation.9 | async-start | bytes 9437184 | tf_op jit(solution)/shard_map/all_gather | solution.py:26
  908.2 131.3 %copy-start.2 = (bf16[128,4,2048]{2,0,1:T(8,128)(2,1)S(1)}, bf16[128,4,2048]{2,0,1:T(8,128)(2,1)}, u32[]{:S(2)}) copy-start(bf16[128,4,2048]{2,0,1:T(8,128)(2,1)} %all-gather.10.cloned.1.call-done) | copy-start | bytes 6291460
  916.2 144.9 %all-gather.24.cloned.1.call-start = ((), (), s32[]{:S(2)}) async-start(), calls=%async_computation.10 | async-start | bytes 1310720 | tf_op jit(solution)/shard_map/all_gather | solution.py:13
  1046.1 79.0 %all-gather.26.cloned.1.call-start = ((), (), s32[]{:S(2)}) async-start(), calls=%async_computation.11 | async-start | bytes 2359296 | tf_op jit(solution)/shard_map/all_gather | solution.py:104
  1061.1 40.1 %all-to-all-start = ((bf16[128,8,512]{0,2,1:T(8,128)(2,1)}), bf16[128,8,512]{0,2,1:T(8,128)(2,1)S(1)}, u32[]{:S(2)}, u32[]{:S(2)}) async-start(bf16[128,8,512]{0,2,1:T(8,128)(2,1)} %bitcast.57), calls=%async_computation.1 | async-start | bytes 2097152 | tf_op jit(solution)/shard_map/all_to_all | solution.py:100
Sparse Core Ops, SparseCore 0:
  10.1 25.2 all-gather.9
  45.5 280.1 reduce-scatter.1
  453.7 34.2 all-gather.15
  490.5 124.9 all-gather.13
  617.4 123.1 all-gather.11
  742.5 32.6 all-gather.17
  783.2 124.9 all-gather.19
  916.3 123.1 all-gather.21
  1046.2 14.8 all-gather.23
  1063.5 61.5 all-gather.25
where the time goes:
time: 1140 us
  waiting for transfers between devices  932 us (82%)
  blocking collectives  120 us (11%)
  matrix products  54.2 us (5%)
  between operations  14.3 us (1%)
    all_gather x4, waiting for transfers between devices, shared_rows(): return lax.all_gather(piece, ('tok', 'grp'), axis=0, tiled=True)  493 us
    reduce_scatter x1, waiting for transfers between devices, token_sums(): lax.psum_scatter(maker(jnp.int32(0), rows * lax.axis_size(('tok', 'grp'))...  280 us
    psum x3, blocking collectives, shared_total(): return lax.psum(vector, ('tok', 'out', 'grp'))  120 us
    all_gather x4, waiting for transfers between devices, spread(): return lax.all_gather(piece, 'out', axis=2, tiled=True)  108 us
    all_to_all x1, waiting for transfers between devices, local(): lax.all_to_all(acts_whole, ('tok', 'grp'), split_axis=1, concat_axis=0, t...  27.3 us
    dot_general x3, matrix products, multiply(): jnp.einsum('rkj,jkc->rkc', row_band, column_band, preferred_element_type=...  23.8 us
  transfers between devices with their start and end apart: 11, of which 11 were waited for; matrix products, arithmetic and copies ran while one was open for 1% of the time, Pallas kernels for 0%

commit v1 on v0

--- a/solution.py
+++ b/solution.py
@@ -27,7 +27,7 @@
 
 
 def shared_total(vector):
-    return lax.psum(vector, ("tok", "out", "grp"))
+    return jnp.sum(lax.all_gather(vector, ("tok", "out", "grp")), axis=0)
 
 
 def diagonal_mask(rows, width, row_start, col_start):

time: 1140 us -> 1180 us (1.035)
  waiting for transfers between devices: 932 us -> 1090 us
  blocking collectives: 120 us -> 0 us
    all_gather x0 -> x3, waiting for transfers between devices: none -> 159 us  [shared_total(): return jnp.sum(lax.all_gather(vector, ('tok', 'out', 'grp')), axis=0)]
    psum x3 -> x0, blocking collectives: 120 us -> none  [shared_total(): return lax.psum(vector, ('tok', 'out', 'grp'))]
  transfers between devices with their start and end apart: 11 -> 14, of which waited for: 11 -> 14; matrix products, arithmetic and copies ran while one was open for 1% -> 1% of each run, Pallas kernels for 0% -> 0%
where the time goes in v1:
time: 1180 us
  waiting for transfers between devices  1090 us (92%)
  matrix products  54.2 us (5%)
  between operations  14 us (1%)
    all_gather x4, waiting for transfers between devices, shared_rows(): return lax.all_gather(piece, ('tok', 'grp'), axis=0, tiled=True)  493 us
    reduce_scatter x1, waiting for transfers between devices, token_sums(): lax.psum_scatter(maker(jnp.int32(0), rows * lax.axis_size(('tok', 'grp'))...  280 us
    all_gather x3, waiting for transfers between devices, shared_total(): return jnp.sum(lax.all_gather(vector, ('tok', 'out', 'grp')), axis=0)  159 us
    all_gather x4, waiting for transfers between devices, spread(): return lax.all_gather(piece, 'out', axis=2, tiled=True)  107 us
    all_to_all x1, waiting for transfers between devices, local(): lax.all_to_all(acts_whole, ('tok', 'grp'), split_axis=1, concat_axis=0, t...  27.3 us
    dot_general x3, matrix products, multiply(): jnp.einsum('rkj,jkc->rkc', row_band, column_band, preferred_element_type=...  23.8 us
  transfers between devices with their start and end apart: 14, of which 14 were waited for; matrix products, arithmetic and copies ran while one was open for 1% of the time, Pallas kernels for 0%

profile of v1, /device:TPU:0, one launch (start us, length us, event | category | flops | bytes accessed | tf_op | source)
XLA Modules:
  0.0 1181.4 jit_solution(15112005716104359299)
XLA Ops:
  7.2 0.0 all-gather.13.cloned.1.call-start
  7.2 1.0 copy_dynamic-update-slice_fusion.1
  8.2 1.0 copy_dynamic-update-slice_fusion
  9.2 0.8 copy-done.1
  10.0 0.0 all-gather.13.cloned.1.call-update
  10.0 0.0 reduce-scatter.2.cloned.1.call-start
  10.0 25.4 %all-gather.13.cloned.1.call-done = bf16[128,4,2048]{2,0,1:T(8,128)(2,1)} async-done(((bf16[128,4,512]{2,0,1:T(8,128)(2,1)}), bf16[128,4,2048]{2,0,1:T(8,128)(2,1)}) %all-gather.13.cloned.1.call-update) | async-done | bytes 2097168 | tf_op jit(solution)/shard_map/all_gather | solution.py:13
  35.4 9.9 convolution_bitcast_fusion
  45.3 0.0 all-gather.15.cloned.1.call-start
  45.4 0.1 select_multiply_fusion.1
  45.5 280.1 %reduce-scatter.2.cloned.1.call-done = f32[256,4,512]{0,2,1:T(8,128)} async-done(((f32[2048,4,512]{0,2,1:T(8,128)}), f32[256,4,512]{0,2,1:T(8,128)}) %reduce-scatter.2.cloned.1.call-update) | async-done | bytes 2097168 | tf_op jit(solution)/shard_map/reduce_scatter | solution.py:17
  325.7 3.0 fusion.10
  328.7 0.6 copy-done.4
  329.4 0.0 all-gather.17.cloned.1.call-start
  329.4 53.0 %all-gather.15.cloned.1.call-done = f32[32,4,2048]{2,1,0:T(4,128)} async-done(((f32[1,4,2048]{2,1,0:T(4,128)}), f32[32,4,2048]{2,1,0:T(4,128)}) %all-gather.15.cloned.1.call-update) | async-done | bytes 1048592 | tf_op jit(solution)/shard_map/all_gather | solution.py:30
  382.4 1.4 reduce_sum.63
  383.8 0.1 multiply_reduce_fusion.3
  383.9 0.1 fusion.26
  384.0 1.3 fusion.9
  385.3 0.6 copy-done.5
  386.0 0.0 all-gather.19.cloned.1.call-start
  386.0 52.8 %all-gather.17.cloned.1.call-done = f32[32,4,2048]{2,1,0:T(4,128)} async-done(((f32[1,4,2048]{2,1,0:T(4,128)}), f32[32,4,2048]{2,1,0:T(4,128)}) %all-gather.17.cloned.1.call-update) | async-done | bytes 1048592 | tf_op jit(solution)/shard_map/all_gather | solution.py:30
  438.9 1.4 reduce_sum.65
  440.3 0.1 multiply_reduce_fusion.2
  440.4 0.1 broadcast_divide_fusion
  440.5 1.3 fusion.8
  441.8 0.6 copy-done.3
  442.5 0.0 all-gather.25.cloned.1.call-start
  442.5 52.8 %all-gather.19.cloned.1.call-done = f32[32,4,2048]{2,1,0:T(4,128)} async-done(((f32[1,4,2048]{2,1,0:T(4,128)}), f32[32,4,2048]{2,1,0:T(4,128)}) %all-gather.19.cloned.1.call-update) | async-done | bytes 1048592 | tf_op jit(solution)/shard_map/all_gather | solution.py:30
  495.4 1.4 reduce_sum.67
  496.8 0.2 multiply_reduce_fusion
  497.0 1.8 multiply_convert_fusion.1
  498.8 0.0 all-gather.25.cloned.1.call-update
  498.8 0.0 all-gather.23.cloned.1.call-start
  498.8 0.7 all-gather.23.cloned.1.call-update
  499.5 0.0 all-gather.21.cloned.1.call-start
  499.6 0.7 all-gather.21.cloned.1.call-update
  500.3 0.0 all-gather.27.cloned.1.call-start
  500.3 32.0 %all-gather.25.cloned.1.call-done = bf16[256,4,2048]{0,2,1:T(8,128)(2,1)} async-done(((bf16[256,4,512]{0,2,1:T(8,128)(2,1)}), bf16[256,4,2048]{0,2,1:T(8,128)(2,1)}) %all-gather.25.cloned.1.call-update) | async-done | bytes 4194320 | tf_op jit(solution)/shard_map/all_gather | solution.py:13
  532.4 127.6 %all-gather.23.cloned.1.call-done = bf16[2048,4,512]{0,2,1:T(8,128)(2,1)} async-done(((bf16[256,4,512]{0,2,1:T(8,128)(2,1)}), bf16[2048,4,512]{0,2,1:T(8,128)(2,1)}) %all-gather.23.cloned.1.call-update) | async-done | bytes 8388624 | tf_op jit(solution)/shard_map/all_gather | solution.py:26
  660.0 7.9 fusion.5
  667.9 0.2 all-gather.29.cloned.1.call-start
  668.1 117.1 %all-gather.21.cloned.1.call-done = bf16[2048,4,512]{0,2,1:T(8,128)(2,1)} async-done(((bf16[256,4,512]{0,2,1:T(8,128)(2,1)}), bf16[2048,4,512]{0,2,1:T(8,128)(2,1)}) %all-gather.21.cloned.1.call-update) | async-done | bytes 8388624 | tf_op jit(solution)/shard_map/all_gather | solution.py:26
  785.2 34.8 %all-gather.27.cloned.1.call-done = bf16[256,4,2048]{0,2,1:T(8,128)(2,1)} async-done(((bf16[256,4,512]{0,2,1:T(8,128)(2,1)}), bf16[256,4,2048]{0,2,1:T(8,128)(2,1)}) %all-gather.27.cloned.1.call-update) | async-done | bytes 4194320 | tf_op jit(solution)/shard_map/all_gather | solution.py:13
  820.0 7.9 fusion.4
  827.9 0.0 all-gather.31.cloned.1.call-start
  827.9 125.0 %all-gather.29.cloned.1.call-done = bf16[2048,4,512]{0,2,1:T(8,128)(2,1)} async-done(((bf16[256,4,512]{0,2,1:T(8,128)(2,1)}), bf16[2048,4,512]{0,2,1:T(8,128)(2,1)}) %all-gather.29.cloned.1.call-update) | async-done | bytes 8388624 | tf_op jit(solution)/shard_map/all_gather | solution.py:26
  953.0 8.0 fusion.6
  961.0 0.0 all-gather.33.cloned.1.call-start
  961.1 123.2 %all-gather.31.cloned.1.call-done = bf16[2048,4,512]{0,2,1:T(8,128)(2,1)} async-done(((bf16[256,4,512]{0,2,1:T(8,128)(2,1)}), bf16[2048,4,512]{0,2,1:T(8,128)(2,1)}) %all-gather.31.cloned.1.call-update) | async-done | bytes 8388624 | tf_op jit(solution)/shard_map/all_gather | solution.py:26
  1084.3 5.7 fusion.11
  1090.0 0.8 fusion.34
  1090.9 0.0 all-gather.35.cloned.1.call-start
  1090.9 0.7 all-gather.35.cloned.1.call-update
  1091.6 14.3 %all-gather.33.cloned.1.call-done = bf16[128,2,2048]{0,2,1:T(8,128)(2,1)} async-done(((bf16[128,2,512]{0,2,1:T(8,128)(2,1)}), bf16[128,2,2048]{0,2,1:T(8,128)(2,1)}) %all-gather.33.cloned.1.call-update) | async-done | bytes 1048592 | tf_op jit(solution)/shard_map/all_gather | solution.py:13
  1105.9 5.5 all-to-all-start
  1111.4 6.3 fusion.15
  1117.7 1.0 copy.31
  1118.6 27.3 %all-to-all-done = bf16[128,8,512]{0,2,1:T(8,128)(2,1)S(1)} async-done(((bf16[128,8,512]{0,2,1:T(8,128)(2,1)}), bf16[128,8,512]{0,2,1:T(8,128)(2,1)S(1)}, u32[]{:S(2)}, u32[]{:S(2)}) %all-to-all-start) | async-done | bytes 1048608 | tf_op jit(solution)/shard_map/all_to_all | solution.py:100
  1146.0 0.7 copy.27
  1146.7 0.5 reshape.87
  1147.2 22.8 %all-gather.35.cloned.1.call-done = bf16[1024,2,512]{0,2,1:T(8,128)(2,1)} async-done(((bf16[128,2,512]{0,2,1:T(8,128)(2,1)}), bf16[1024,2,512]{0,2,1:T(8,128)(2,1)}) %all-gather.35.cloned.1.call-update) | async-done | bytes 2097168 | tf_op jit(solution)/shard_map/all_gather | solution.py:104
  1170.0 2.9 multiply_convert_fusion
  1172.9 2.0 copy.30
  (28 shorter events, 0.3 us)
Async XLA Ops:
  7.2 28.3 %all-gather.13.cloned.1.call-start = ((), (), s32[]{:S(2)}) async-start(), calls=%async_computation.2 | async-start | bytes 2621440 | tf_op jit(solution)/shard_map/all_gather | solution.py:13
  9.2 0.8 copy-start.1
  10.0 315.7 %reduce-scatter.2.cloned.1.call-start = ((), (), s32[]{:S(2)}) async-start(), calls=%async_computation.3 | async-start | bytes 18874368 | tf_op jit(solution)/shard_map/reduce_scatter | solution.py:17
  45.3 337.1 %all-gather.15.cloned.1.call-start = ((), (), s32[]{:S(2)}) async-start(), calls=%async_computation.4 | async-start | bytes 1081344 | tf_op jit(solution)/shard_map/all_gather | solution.py:30
  325.7 58.3 %copy-start = (f32[256,4,512]{0,2,1:T(8,128)S(1)}, f32[256,4,512]{0,2,1:T(8,128)}, u32[]{:S(2)}) copy-start(f32[256,4,512]{0,2,1:T(8,128)} %reduce-scatter.2.cloned.1.call-done) | copy-start | bytes 6291460
  328.7 0.6 copy-start.4
  329.4 109.5 %all-gather.17.cloned.1.call-start = ((), (), s32[]{:S(2)}) async-start(), calls=%async_computation.5 | async-start | bytes 1081344 | tf_op jit(solution)/shard_map/all_gather | solution.py:30
  385.3 0.6 copy-start.5
  386.0 109.4 %all-gather.19.cloned.1.call-start = ((), (), s32[]{:S(2)}) async-start(), calls=%async_computation.6 | async-start | bytes 1081344 | tf_op jit(solution)/shard_map/all_gather | solution.py:30
  441.8 0.6 copy-start.3
  442.5 89.9 %all-gather.25.cloned.1.call-start = ((), (), s32[]{:S(2)}) async-start(), calls=%async_computation.9 | async-start | bytes 5242880 | tf_op jit(solution)/shard_map/all_gather | solution.py:13
  498.8 161.2 %all-gather.23.cloned.1.call-start = ((), (), s32[]{:S(2)}) async-start(), calls=%async_computation.8 | async-start | bytes 9437184 | tf_op jit(solution)/shard_map/all_gather | solution.py:26
  499.5 285.6 %all-gather.21.cloned.1.call-start = ((), (), s32[]{:S(2)}) async-start(), calls=%async_computation.7 | async-start | bytes 9437184 | tf_op jit(solution)/shard_map/all_gather | solution.py:26
  500.3 319.7 %all-gather.27.cloned.1.call-start = ((), (), s32[]{:S(2)}) async-start(), calls=%async_computation.10 | async-start | bytes 5242880 | tf_op jit(solution)/shard_map/all_gather | solution.py:13
  667.9 285.1 %all-gather.29.cloned.1.call-start = ((), (), s32[]{:S(2)}) async-start(), calls=%async_computation.11 | async-start | bytes 9437184 | tf_op jit(solution)/shard_map/all_gather | solution.py:26
  827.9 256.4 %all-gather.31.cloned.1.call-start = ((), (), s32[]{:S(2)}) async-start(), calls=%async_computation.12 | async-start | bytes 9437184 | tf_op jit(solution)/shard_map/all_gather | solution.py:26
  953.0 131.3 %copy-start.2 = (bf16[128,4,2048]{2,0,1:T(8,128)(2,1)S(1)}, bf16[128,4,2048]{2,0,1:T(8,128)(2,1)}, u32[]{:S(2)}) copy-start(bf16[128,4,2048]{2,0,1:T(8,128)(2,1)} %all-gather.13.cloned.1.call-done) | copy-start | bytes 6291460
  961.0 144.9 %all-gather.33.cloned.1.call-start = ((), (), s32[]{:S(2)}) async-start(), calls=%async_computation.13 | async-start | bytes 1310720 | tf_op jit(solution)/shard_map/all_gather | solution.py:13
  1090.9 79.1 %all-gather.35.cloned.1.call-start = ((), (), s32[]{:S(2)}) async-start(), calls=%async_computation.14 | async-start | bytes 2359296 | tf_op jit(solution)/shard_map/all_gather | solution.py:104
  1105.9 40.1 %all-to-all-start = ((bf16[128,8,512]{0,2,1:T(8,128)(2,1)}), bf16[128,8,512]{0,2,1:T(8,128)(2,1)S(1)}, u32[]{:S(2)}, u32[]{:S(2)}) async-start(bf16[128,8,512]{0,2,1:T(8,128)(2,1)} %bitcast.60), calls=%async_computation.1 | async-start | bytes 2097152 | tf_op jit(solution)/shard_map/all_to_all | solution.py:100
Sparse Core Ops, SparseCore 0:
  10.1 25.2 all-gather.12
  45.4 280.1 reduce-scatter.1
  329.5 52.8 all-gather.14
  386.1 52.7 all-gather.16
  442.6 52.7 all-gather.18
  498.9 33.4 all-gather.24
  535.0 124.9 all-gather.22
  662.0 123.1 all-gather.20
  787.3 32.6 all-gather.26
  828.0 124.9 all-gather.28
  961.1 123.1 all-gather.30
  1091.0 14.8 all-gather.32
  1108.5 61.4 all-gather.34
